TPU v7x, 128 devices: a whole 4x4x4 slice. The times are simulated.
128 devices in a mesh: grp: 2 (over x_lo), wide: 64 (over z, x_hi, y, core).
Axes of the slice: x: 4 (x_hi: 2, x_lo: 2; x = x_hi * 2 + x_lo), y: 4, z: 4, core: 2. Of those that a mesh axis runs over, the one named last changes fastest.
Arguments:
- x_pool: bfloat16 [65536, 7168], P(('grp', 'wide')), may hold values from -6 to 6
- token_ids: int32 [16384], P(('grp', 'wide')), may hold values from 0 to 65535, as said below
- cotangent: bfloat16 [16384, 7168], P(('grp', 'wide')), may hold values from -6 to 6
- gate_up: bfloat16 [2, 1024, 7168], P(None, 'wide', 'grp'), may hold values from -0.0625 to 0.0625
- down_weight: bfloat16 [1024, 7168], P('wide', 'grp'), may hold values from -0.1875 to 0.1875
- loss_exponent: int32 [1], replicated, may hold values from 3 to 9
Outputs:
- grad_gate_up: bfloat16 [2, 1024, 7168], P(None, 'wide', 'grp')
- grad_down: bfloat16 [1024, 7168], P('wide', 'grp')
Inputs may be any that keep to these rules, and one draw needn't show every extreme that they name: The 128 ids in aligned block b of token_ids name rows b * 512 to (b + 1) * 512 - 1 of x_pool.
All inputs are finite; a program needn't handle non-finite values.
Results may differ from a plain program's by a relative error of at most 0.014.
Values may be sent and summed in bfloat16 or wider, within the bound.
A program may use at most 192 MiB of HBM per device.

v0:
```python
import jax
import jax.numpy as jnp
import numpy as np
from jax import lax
from jax.sharding import PartitionSpec as P

BLOCKS = 8


def swapped(value, axis, bit):
    mask = 2**bit
    pairs = [(source, source ^ mask) for source in range(lax.axis_size(axis))]
    return lax.ppermute(value, axis, pairs)


def sent_to_all(x, axis):
    copies = jnp.broadcast_to(x, (lax.axis_size(axis), *x.shape))
    return lax.all_to_all(copies, axis, split_axis=0, concat_axis=0, tiled=True)


def in_order(parts, dim):
    shape = list(parts.shape[1:])
    shape[dim] *= parts.shape[0]
    return jnp.moveaxis(parts, 0, dim).reshape(shape)


def gather_directly(x, axis, dim):
    parts = sent_to_all(x, axis)
    return in_order(parts, dim)


def split_up(x, dim, devices):
    before, after = (x.shape[:dim], x.shape[dim + 1 :])
    return jnp.moveaxis(x.reshape(*before, devices, -1, *after), dim, 0)


def summed_on_arrival(x, axis, dim):
    devices = lax.axis_size(axis)
    parts = lax.all_to_all(split_up(x, dim, devices), axis, 0, 0, tiled=True)
    return jnp.sum(parts.astype(jnp.float32), axis=0)


def unscale_of(loss_exponent):
    levels = jnp.arange(16, dtype=jnp.int32)
    powers = jnp.asarray(np.power(0.5, np.arange(16)), dtype=jnp.float32)
    return jnp.sum(jnp.where(levels == loss_exponent[0], powers, jnp.float32(0.0)))


def contract_last(left_side, right_side):
    return lax.dot_general(
        left_side, right_side, (((1,), (1,)), ((), ())), preferred_element_type=jnp.float32
    )


def contract_first(left_side, right_side):
    return lax.dot_general(
        left_side, right_side, (((0,), (0,)), ((), ())), preferred_element_type=jnp.float32
    )


def halve_blocks(gradients, wide_index, low_bits):
    for bit_index in reversed(range(low_bits)):
        half_units = gradients.shape[1] // 2
        lower_half = gradients[:, :half_units]
        upper_half = gradients[:, half_units:]
        own_bit = wide_index >> bit_index & 1
        kept_half = jnp.where(own_bit == 0, lower_half, upper_half)
        sent_half = jnp.where(own_bit == 0, upper_half, lower_half).astype(jnp.bfloat16)
        arrived = swapped(sent_half, "wide", bit_index)
        gradients = kept_half + arrived.astype(jnp.float32)
    return gradients


def per_device(x_pool, token_ids, cotangent, gate_up, down_weight, loss_exponent):
    wide_count = lax.axis_size("wide")
    group_count = wide_count // BLOCKS
    low_bits = group_count.bit_length() - 1
    all_bits = wide_count.bit_length() - 1
    wide_index = lax.axis_index("wide")
    device_index = lax.axis_index("grp") * wide_count + wide_index
    local_rows = token_ids - device_index * x_pool.shape[0]
    picked = jnp.take(x_pool, local_rows, axis=0)
    stacked = jnp.stack([picked, cotangent])
    model_width = stacked.shape[2]
    weight_tile = jnp.concatenate([gate_up, down_weight[None]], axis=0)
    weight_rows = gather_directly(weight_tile, "grp", 2)
    for bit_index in range(low_bits):
        partner = swapped(weight_rows, "wide", bit_index)
        own_bit = wide_index >> bit_index & 1
        weight_rows = jnp.where(
            own_bit == 0,
            jnp.concatenate([weight_rows, partner], axis=1),
            jnp.concatenate([partner, weight_rows], axis=1),
        )
    hidden_units = weight_rows.shape[1]
    gathered = stacked
    for bit_index in range(low_bits, all_bits):
        partner_tokens = swapped(gathered, "wide", bit_index)
        gathered = jnp.concatenate([gathered, partner_tokens], axis=1)
    tokens_in = gathered[0]
    tokens_grad = gathered[1]
    unscale = unscale_of(loss_exponent)
    gate_up_rows = weight_rows[:2].reshape(2 * hidden_units, model_width)
    projected = contract_last(tokens_in, gate_up_rows)
    gate_act = projected[:, :hidden_units]
    up_act = projected[:, hidden_units:]
    delta_hidden = unscale * contract_last(tokens_grad, weight_rows[2])
    sigmoid_gate = jax.nn.sigmoid(gate_act)
    hidden = (gate_act * sigmoid_gate * up_act).astype(jnp.bfloat16)
    delta_gate = (
        delta_hidden * up_act * sigmoid_gate * (1.0 + gate_act * (1.0 - sigmoid_gate))
    ).astype(jnp.bfloat16)
    delta_up = (delta_hidden * gate_act * sigmoid_gate).astype(jnp.bfloat16)
    delta_pair = jnp.concatenate([delta_gate, delta_up], axis=1)
    grad_pair = contract_first(delta_pair, tokens_in)
    grad_hidden = unscale * contract_first(hidden, tokens_grad)
    gradients = jnp.concatenate([grad_pair, grad_hidden], axis=0).reshape(
        3, hidden_units, model_width
    )
    gradients = halve_blocks(gradients, wide_index, low_bits)
    gradients = summed_on_arrival(gradients.astype(jnp.bfloat16), "grp", 2)
    finished = gradients.astype(jnp.bfloat16)
    return (finished[:2], finished[2])


def solution(mesh):
    in_specs = (
        P(("grp", "wide"), None),
        P(("grp", "wide")),
        P(("grp", "wide"), None),
        P(None, "wide", "grp"),
        P("wide", "grp"),
        P(),
    )
    out_specs = (P(None, "wide", "grp"), P("wide", "grp"))
    return jax.shard_map(
        per_device, mesh=mesh, in_specs=in_specs, out_specs=out_specs, check_vma=False
    )
```

profile of v0, /device:TPU:0, one launch (start us, length us, event | category | flops | bytes accessed | tf_op | source)
XLA Modules:
  0.0 770.6 jit_solution(5681750495153580750)
XLA Ops:
  1.3 8.7 %gather_fusion = bf16[128,7168]{1,0:T(8,128)(2,1)} fusion(bf16[512,7168]{1,0:T(8,128)(2,1)} %param.7, s32[1024]{0:T(1024)S(1)} %pad_clamp_fusion), kind=kCustom, calls=%fused_computation | custom fusion | bytes 3670528 | tf_op jit(solution)/shard_map/jit(_take)/gather | solution.py:82
  10.0 1.9 bitcast_select_fusion
  11.8 1.8 pad_maximum_fusion.4
  13.7 3.2 collective-permute-start
  16.9 79.3 %collective-permute-done = bf16[2,128,7168]{2,1,0:T(8,128)(2,1)S(1)} collective-permute-done((bf16[2,128,7168]{2,1,0:T(8,128)(2,1)S(1)}, bf16[2,128,7168]{2,1,0:T(8,128)(2,1)S(1)}, u32[]{:S(2)}, u32[]{:S(2)}) %collective-permute-start) | collective-permute-done | bytes 3670048 | tf_op jit(solution)/shard_map/ppermute | solution.py:13
  96.9 2.2 collective-permute-start.1
  99.1 157.1 %collective-permute-done.1 = bf16[2,256,7168]{2,1,0:T(8,128)(2,1)S(1)} collective-permute-done((bf16[2,256,7168]{2,1,0:T(8,128)(2,1)S(1)}, bf16[2,256,7168]{2,1,0:T(8,128)(2,1)S(1)}, u32[]{:S(2)}, u32[]{:S(2)}) %collective-permute-start.1) | collective-permute-done | bytes 7340064 | tf_op jit(solution)/shard_map/ppermute | solution.py:13
  256.2 7.9 %pad_maximum_fusion.1 = bf16[2,512,7168]{2,1,0:T(8,128)(2,1)} fusion(bf16[2,256,7168]{2,1,0:T(8,128)(2,1)S(1)} %collective-permute-done.1, bf16[2,128,7168]{2,1,0:T(8,128)(2,1)S(1)} %collective-permute-done, bf16[1,128,7168]{2,1,0:T(8,128)(2,1)S(1)} %bitcast.41, bf16[1,128,7168]{2,1,0:T(8,128)(2,1)S(1)} %bitcast_select_fusion), kind=kLoop, calls=%fused_computation.4 | loop fusion | flops 58720256 | bytes 29360128 | tf_op jit(solution)/shard_map/concatenate | solution.py:99
  264.1 3.7 collective-permute-start.2
  267.9 10.4 %all_to_all.10 = bf16[2,3,16,3584]{3,2,1,0:T(8,128)(2,1)S(1)} all-to-all(bf16[2,3,16,3584]{3,2,1,0:T(8,128)(2,1)S(1)} %broadcast_in_dim.27), channel_id=1, replica_groups=mesh['grp'=2,'wide'=64] {'grp'}, dimensions={0} | all-to-all | bytes 1376256 | tf_op jit(solution)/shard_map/all_to_all | solution.py:18
  280.8 2.1 maximum_select_fusion.2
  284.5 30.8 %collective-permute-done.4 = bf16[3,32,7168]{2,1,0:T(8,128)(2,1)} collective-permute-done((bf16[3,32,7168]{2,1,0:T(8,128)(2,1)S(1)}, bf16[3,32,7168]{2,1,0:T(8,128)(2,1)}, u32[]{:S(2)}, u32[]{:S(2)}) %collective-permute-start.4) | collective-permute-done | bytes 1376288 | tf_op jit(solution)/shard_map/ppermute | solution.py:13
  315.3 3.3 maximum_select_fusion.1
  318.6 3.2 collective-permute-start.5
  323.0 58.2 %collective-permute-done.5 = bf16[3,64,7168]{2,1,0:T(8,128)(2,1)} collective-permute-done((bf16[3,64,7168]{2,1,0:T(8,128)(2,1)}, bf16[3,64,7168]{2,1,0:T(8,128)(2,1)}, u32[]{:S(2)}, u32[]{:S(2)}) %collective-permute-start.5) | collective-permute-done | bytes 2752544 | tf_op jit(solution)/shard_map/ppermute | solution.py:13
  381.3 6.1 maximum_select_fusion
  387.4 2.4 copy-done.3
  389.8 2.2 slice.61
  391.9 189.8 %collective-permute-done.2 = bf16[2,512,7168]{2,1,0:T(8,128)(2,1)} collective-permute-done((bf16[2,512,7168]{2,1,0:T(8,128)(2,1)}, bf16[2,512,7168]{2,1,0:T(8,128)(2,1)}, u32[]{:S(2)}, u32[]{:S(2)}) %collective-permute-start.2) | collective-permute-done | bytes 14680096 | tf_op jit(solution)/shard_map/ppermute | solution.py:13
  581.7 19.6 %pad_maximum_fusion = bf16[2,1024,7168]{2,1,0:T(8,128)(2,1)} fusion(bf16[2,512,7168]{2,1,0:T(8,128)(2,1)} %collective-permute-done.2, bf16[2,256,7168]{2,1,0:T(8,128)(2,1)} %copy-done.2, bf16[2,128,7168]{2,1,0:T(8,128)(2,1)} %copy-done, bf16[1,128,7168]{2,1,0:T(8,128)(2,1)} %bitcast.39, bf16[1,128,7168]{2,1,0:T(8,128)(2,1)S(1)} %bitcast_select_fusion), kind=kLoop, calls=%fused_computation.1 | loop fusion | flops 146800640 | bytes 58720256 | tf_op jit(solution)/shard_map/concatenate | solution.py:99
  601.3 8.5 %fusion.3 = f32[1024,256]{0,1:T(8,128)S(1)} fusion(bf16[256,7168]{1,0:T(8,128)(2,1)} %bitcast.42, bf16[2,1024,7168]{2,1,0:T(8,128)(2,1)} %pad_maximum_fusion), kind=kOutput, calls=%fused_computation.8 | convolution fusion | flops 3758096384 | bytes 19398656 | tf_op jit(solution)/shard_map/dot_general | solution.py:50
  609.9 11.4 %multiply_convert_fusion.2 = (bf16[1024,128]{0,1:T(8,128)(2,1)S(1)}, bf16[1024,128]{0,1:T(8,128)(2,1)S(1)}) fusion(f32[1024,256]{0,1:T(8,128)S(1)} %fusion.3, bf16[3,128,7168]{2,1,0:T(8,128)(2,1)} %copy-done.3, bf16[2,1024,7168]{2,1,0:T(8,128)(2,1)} %pad_maximum_fusion, f32[]{:T(128)} %fusion.10), kind=kOutput, calls=%fused_computation.30 | convolution fusion | flops 1880883200 | bytes 18088448 | tf_op jit(solution)/shard_map/dot_general | solution.py:50
  621.3 9.8 %fusion.4 = f32[128,7168]{1,0:T(8,128)} fusion(bf16[2,1024,7168]{2,1,0:T(8,128)(2,1)} %pad_maximum_fusion, f32[]{:T(128)} %fusion.10, f32[1024,256]{0,1:T(8,128)S(1)} %fusion.3), kind=kOutput, calls=%fused_computation.10 | convolution fusion | flops 1880752128 | bytes 19399168 | tf_op jit(solution)/shard_map/dot_general | solution.py:56
  631.1 12.1 %fusion.2 = f32[256,7168]{1,0:T(8,128)} fusion(bf16[2,1024,7168]{2,1,0:T(8,128)(2,1)} %pad_maximum_fusion, bf16[1024,128]{0,1:T(8,128)(2,1)S(1)} %get-tuple-element.5, bf16[1024,128]{0,1:T(8,128)(2,1)S(1)} %get-tuple-element.4), kind=kOutput, calls=%fused_computation.7 | convolution fusion | flops 3759144960 | bytes 22544384 | tf_op jit(solution)/shard_map/dot_general | solution.py:56
  643.2 9.6 %pad_maximum_fusion.2 = f32[384,7168]{1,0:T(8,128)} fusion(f32[128,7168]{1,0:T(8,128)} %fusion.4, f32[256,7168]{1,0:T(8,128)} %fusion.2), kind=kLoop, calls=%fused_computation.9 | loop fusion | flops 2752512 | bytes 22020096 | tf_op jit(solution)/shard_map/concatenate | solution.py:117
  652.8 4.7 select_convert_fusion
  657.4 3.3 collective-permute-start.6
  660.7 57.4 %collective-permute-done.6 = bf16[3,64,7168]{2,1,0:T(8,128)(2,1)S(1)} collective-permute-done((bf16[3,64,7168]{2,1,0:T(8,128)(2,1)S(1)}, bf16[3,64,7168]{2,1,0:T(8,128)(2,1)S(1)}, u32[]{:S(2)}, u32[]{:S(2)}) %collective-permute-start.6) | collective-permute-done | bytes 2752544 | tf_op jit(solution)/shard_map/ppermute | solution.py:13
  718.1 5.4 convert_add_fusion
  725.4 27.2 %collective-permute-done.7 = bf16[3,32,7168]{2,1,0:T(8,128)(2,1)S(1)} collective-permute-done((bf16[3,32,7168]{2,1,0:T(8,128)(2,1)S(1)}, bf16[3,32,7168]{2,1,0:T(8,128)(2,1)S(1)}, u32[]{:S(2)}, u32[]{:S(2)}) %collective-permute-start.7) | collective-permute-done | bytes 1376288 | tf_op jit(solution)/shard_map/ppermute | solution.py:13
  753.4 2.1 collective-permute-done.8
  756.3 12.7 %all_to_all.11 = bf16[2,3,16,3584]{3,2,1,0:T(8,128)(2,1)S(1)} all-to-all(bf16[2,3,16,3584]{3,2,1,0:T(8,128)(2,1)S(1)} %copy.10), channel_id=1, replica_groups=mesh['grp'=2,'wide'=64] {'grp'}, dimensions={0} | all-to-all | bytes 1376256 | tf_op jit(solution)/shard_map/all_to_all | solution.py:39
  (36 shorter events, 11.0 us)
Async XLA Ops:
  10.0 86.3 %copy-start.1 = (bf16[128,7168]{1,0:T(8,128)(2,1)S(1)}, bf16[128,7168]{1,0:T(8,128)(2,1)}, u32[]{:S(2)}) copy-start(bf16[128,7168]{1,0:T(8,128)(2,1)} %param.9) | copy-start | bytes 5505028
  13.7 82.6 %collective-permute-start = (bf16[2,128,7168]{2,1,0:T(8,128)(2,1)S(1)}, bf16[2,128,7168]{2,1,0:T(8,128)(2,1)S(1)}, u32[]{:S(2)}, u32[]{:S(2)}) collective-permute-start(bf16[2,128,7168]{2,1,0:T(8,128)(2,1)S(1)} %pad_maximum_fusion.4), channel_id=1, source_target_pairs={{0,8},{1,9},{2,10},{3,11},{4,12},{5,13},{6,14},{7,15},{8,0},{9,1},... | collective-permute-start | bytes 11010056 | tf_op jit(solution)/shard_map/ppermute | solution.py:13
  96.2 160.0 %copy-start = (bf16[2,128,7168]{2,1,0:T(8,128)(2,1)}, bf16[2,128,7168]{2,1,0:T(8,128)(2,1)S(1)}, u32[]{:S(2)}) copy-start(bf16[2,128,7168]{2,1,0:T(8,128)(2,1)S(1)} %collective-permute-done) | copy-start | bytes 11010052
  96.8 171.0 %copy-start.5 = (bf16[2,16,3584]{2,1,0:T(8,128)(2,1)S(1)}, bf16[2,16,3584]{2,1,0:T(8,128)(2,1)}, u32[]{:S(2)}) copy-start(bf16[2,16,3584]{2,1,0:T(8,128)(2,1)} %param.10) | copy-start | bytes 688132
  96.9 171.0 %copy-start.6 = (bf16[16,3584]{1,0:T(8,128)(2,1)S(1)}, bf16[16,3584]{1,0:T(8,128)(2,1)}, u32[]{:S(2)}) copy-start(bf16[16,3584]{1,0:T(8,128)(2,1)} %param.11) | copy-start | bytes 344068
  96.9 159.3 %collective-permute-start.1 = (bf16[2,256,7168]{2,1,0:T(8,128)(2,1)S(1)}, bf16[2,256,7168]{2,1,0:T(8,128)(2,1)S(1)}, u32[]{:S(2)}, u32[]{:S(2)}) collective-permute-start(bf16[2,256,7168]{2,1,0:T(8,128)(2,1)S(1)} %pad_maximum_fusion.3), channel_id=1, source_target_pairs={{0,16},{1,17},{2,18},{3,19},{4,20},{5,21},{6,22},{7,23},{8,24},{9,... | collective-permute-start | bytes 22020104 | tf_op jit(solution)/shard_map/ppermute | solution.py:13
  256.2 7.9 %copy-start.2 = (bf16[2,256,7168]{2,1,0:T(8,128)(2,1)}, bf16[2,256,7168]{2,1,0:T(8,128)(2,1)S(1)}, u32[]{:S(2)}) copy-start(bf16[2,256,7168]{2,1,0:T(8,128)(2,1)S(1)} %collective-permute-done.1) | copy-start | bytes 22020100
  264.1 317.6 %collective-permute-start.2 = (bf16[2,512,7168]{2,1,0:T(8,128)(2,1)}, bf16[2,512,7168]{2,1,0:T(8,128)(2,1)}, u32[]{:S(2)}, u32[]{:S(2)}) collective-permute-start(bf16[2,512,7168]{2,1,0:T(8,128)(2,1)} %pad_maximum_fusion.1), channel_id=1, source_target_pairs={{0,32},{1,33},{2,34},{3,35},{4,36},{5,37},{6,38},{7,39},{8,40},{9,... | collective-permute-start | bytes 44040200 | tf_op jit(solution)/shard_map/ppermute | solution.py:13
  267.9 54.5 %copy-start.7 = (f32[16]{0:T(128)S(1)}, f32[16]{0:T(128)}, u32[]{:S(2)}) copy-start(f32[16]{0:T(128)} %constant.41.clone) | copy-start | bytes 196
  278.4 0.9 copy-start.4
  278.4 2.4 collective-permute-start.3
  282.9 32.4 %collective-permute-start.4 = (bf16[3,32,7168]{2,1,0:T(8,128)(2,1)S(1)}, bf16[3,32,7168]{2,1,0:T(8,128)(2,1)}, u32[]{:S(2)}, u32[]{:S(2)}) collective-permute-start(bf16[3,32,7168]{2,1,0:T(8,128)(2,1)S(1)} %maximum_select_fusion.2), channel_id=1, source_target_pairs={{0,2},{1,3},{2,0},{3,1},{4,6},{5,7},{6,4},{7,5},{8,10},{9,11},{10,... | collective-permute-start | bytes 4128776 | tf_op jit(solution)/shard_map/ppermute | solution.py:13
  318.6 62.7 %collective-permute-start.5 = (bf16[3,64,7168]{2,1,0:T(8,128)(2,1)}, bf16[3,64,7168]{2,1,0:T(8,128)(2,1)}, u32[]{:S(2)}, u32[]{:S(2)}) collective-permute-start(bf16[3,64,7168]{2,1,0:T(8,128)(2,1)} %maximum_select_fusion.1), channel_id=1, source_target_pairs={{0,4},{1,5},{2,6},{3,7},{4,0},{5,1},{6,2},{7,3},{8,12},{9,13},{10,... | collective-permute-start | bytes 8257544 | tf_op jit(solution)/shard_map/ppermute | solution.py:13
  387.4 2.4 copy-start.3
  657.4 60.7 %collective-permute-start.6 = (bf16[3,64,7168]{2,1,0:T(8,128)(2,1)S(1)}, bf16[3,64,7168]{2,1,0:T(8,128)(2,1)S(1)}, u32[]{:S(2)}, u32[]{:S(2)}) collective-permute-start(bf16[3,64,7168]{2,1,0:T(8,128)(2,1)S(1)} %select_convert_fusion), channel_id=1, source_target_pairs={{0,4},{1,5},{2,6},{3,7},{4,0},{5,1},{6,2},{7,3},{8,12},{9,13},{10,... | collective-permute-start | bytes 8257544 | tf_op jit(solution)/shard_map/ppermute | solution.py:13
  723.8 28.9 %collective-permute-start.7 = (bf16[3,32,7168]{2,1,0:T(8,128)(2,1)S(1)}, bf16[3,32,7168]{2,1,0:T(8,128)(2,1)S(1)}, u32[]{:S(2)}, u32[]{:S(2)}) collective-permute-start(bf16[3,32,7168]{2,1,0:T(8,128)(2,1)S(1)} %select_convert_fusion.1), channel_id=1, source_target_pairs={{0,2},{1,3},{2,0},{3,1},{4,6},{5,7},{6,4},{7,5},{8,10},{9,11},{10,... | collective-permute-start | bytes 4128776 | tf_op jit(solution)/shard_map/ppermute | solution.py:13
  753.3 2.2 collective-permute-start.8
where the time goes:
time: 771 us
  waiting for transfers between devices  603 us (78%)
  other arithmetic  65.6 us (9%)
  matrix products  41.8 us (5%)
  blocking collectives  23.1 us (3%)
  starting transfers between devices  19.1 us (2%)
  local copies, waits for them, and re-layouts  16 us (2%)
    ppermute x9, waiting for transfers between devices, swapped(): return lax.ppermute(value, axis, pairs)  603 us
    concatenate x3, other arithmetic, per_device(): gathered = jnp.concatenate([gathered, partner_tokens], axis=1)  28.1 us
    dot_general x2, matrix products, contract_first(): lax.dot_general(left_side, right_side, (((0,), (0,)), ((), ())), preferre...  21.9 us
    dot_general x2, matrix products, contract_last(): lax.dot_general(left_side, right_side, (((1,), (1,)), ((), ())), preferre...  19.9 us
    ppermute x9, starting transfers between devices, swapped(): return lax.ppermute(value, axis, pairs)  19.1 us
  transfers between devices with their start and end apart: 9, of which 9 were waited for; matrix products, arithmetic and copies ran while one was open for 2% of the time, Pallas kernels for 0%

commit v1 on v0

v1 whole, which is shorter than its diff:
```python
import functools

import jax
import jax.numpy as jnp
from jax import lax
from jax.experimental import pallas as pl
from jax.experimental.pallas import tpu as pltpu
from jax.sharding import PartitionSpec as P

MESH = pl.DeviceIdType.MESH
BF16 = jnp.bfloat16
F32 = jnp.float32
COPIES = 128
LOCALS = 16


def dot_nt(a, b):
    return lax.dot_general(a, b, (((1,), (1,)), ((), ())), preferred_element_type=F32)


def dot_nn(a, b):
    return lax.dot_general(a, b, (((1,), (0,)), ((), ())), preferred_element_type=F32)


class Wire:
    def __init__(self, send_sems, recv_sems):
        self.send_sems, self.recv_sems = send_sems, recv_sems
        self.count = 0
        self.sent = []

    def send(self, src, dst, device):
        copy = pltpu.make_async_remote_copy(
            src_ref=src,
            dst_ref=dst,
            send_sem=self.send_sems.at[self.count],
            recv_sem=self.recv_sems.at[self.count],
            device_id=device,
            device_id_type=MESH,
        )
        self.count += 1
        copy.start()
        self.sent.append(copy)
        return copy

    def drain(self):
        for copy in self.sent:
            copy.wait_send()


def kernel(
    pool, ids, cot, gate_up, down, exponent,
    out_pair, out_down,
    tok_x, tok_c, via_x, via_c, picked, pool_q, weights,
    part, part_own, r1p, r1m, r2p, r2m, deltas, grads,
    ra1p, ra1m, ra2p, ra2m, sum_a, ya1p, ya1m, ya2p, ya2m,
    yb1p, yb1m, yb2p, yb2m, sum_b, zb1p, zb1m, zb2p, zb2m,
    final, crossed, send_sems, recv_sems, local_sems,
):
    tokens, width = cot.shape
    quarter = width // 4
    half = quarter // 2
    own_rows = down.shape[0]
    pair_rows = 2 * own_rows
    chunk_rows = 4 * pair_rows
    chip_tokens = 2 * tokens
    pool_rows = pool.shape[0]
    tile = 256 if quarter % 256 == 0 else quarter

    x_lo = lax.axis_index("grp")
    wide = lax.axis_index("wide")
    z = lax.div(wide, 16)
    x_hi = lax.rem(lax.div(wide, 8), 2)
    y = lax.rem(lax.div(wide, 2), 4)
    core = lax.rem(wide, 2)
    x = 2 * x_hi + x_lo
    device_index = x_lo * 64 + wide

    def shift(v, by):
        return lax.rem(v + (by % 4), 4)

    def device(xx, yy, zz, cc):
        return (lax.rem(xx, 2), zz * 16 + lax.div(xx, 2) * 8 + yy * 2 + cc)

    xn, xf, xb = shift(x, 1), shift(x, 2), shift(x, -1)
    yn, yf, yb = shift(y, 1), shift(y, 2), shift(y, -1)
    zn, zf, zb = shift(z, 1), shift(z, 2), shift(z, -1)
    x_next, x_far, x_back = (device(v, y, z, core) for v in (xn, xf, xb))
    y_next, y_back = (device(x, v, z, core) for v in (yn, yb))
    z_next, z_back = (device(x, y, v, core) for v in (zn, zb))
    partner = device(x, y, z, 1 - core)

    def feature_quarter(xx):
        return 2 * lax.rem(xx, 2) + lax.div(xx, 2)

    def q_cols(xx):
        return pl.ds(pl.multiple_of(feature_quarter(xx) * quarter, quarter), quarter)

    def slot(xx, cc):
        return pl.ds(pl.multiple_of((2 * xx + cc) * tokens, tokens), tokens)

    def chip_slot(xx):
        return pl.ds(pl.multiple_of(xx * chip_tokens, chip_tokens), chip_tokens)

    def rows_of(yy):
        return pl.ds(pl.multiple_of(yy * pair_rows, pair_rows), pair_rows)

    def low_rows_of(yy):
        return pl.ds(pl.multiple_of(yy * pair_rows, own_rows), own_rows)

    def high_rows_of(yy):
        return pl.ds(pl.multiple_of(yy * pair_rows + own_rows, own_rows), own_rows)

    def owner_rows(xh):
        return pl.ds(pl.multiple_of(y * pair_rows + xh * own_rows, own_rows), own_rows)

    cols_a = pl.ds(0, half)
    cols_b = pl.ds(half, half)
    all_p = pl.ds(0, 3)
    wire = Wire(send_sems, recv_sems)
    locals_used = [0]

    def fetch(src, dst):
        copy = pltpu.make_async_copy(src, dst, local_sems.at[locals_used[0]])
        locals_used[0] += 1
        copy.start()
        return copy

    far_pool = fetch(pool.at[:, q_cols(xf)], pool_q.at[0])

    barrier = pltpu.get_barrier_semaphore()
    for peer in (x_next, x_back, x_far, y_next, y_back, z_next, z_back, partner):
        pl.semaphore_signal(barrier, inc=1, device_id=peer, device_id_type=MESH)
    pl.semaphore_wait(barrier, 8)

    x_hi_cols = pl.ds(pl.multiple_of(x_hi * quarter, quarter), quarter)
    other_cols = pl.ds(pl.multiple_of((1 - x_hi) * quarter, quarter), quarter)
    wx_pair = wire.send(
        gate_up.at[:, :, other_cols], weights.at[z, pl.ds(0, 2), owner_rows(x_hi), :], x_far
    )
    wx_down = wire.send(down.at[:, other_cols], weights.at[z, 2, owner_rows(x_hi), :], x_far)
    w_pair = fetch(gate_up.at[:, :, x_hi_cols], weights.at[z, pl.ds(0, 2), owner_rows(x_hi), :])
    w_down = fetch(down.at[:, x_hi_cols], weights.at[z, 2, owner_rows(x_hi), :])

    c_via = wire.send(cot.at[:, q_cols(xf)], via_c, x_back)
    c_back = wire.send(cot.at[:, q_cols(xb)], tok_c.at[slot(x, core), :], x_back)
    c_own = fetch(cot.at[:, q_cols(x)], tok_c.at[slot(x, core), :])
    next_pool = fetch(pool.at[:, q_cols(xn)], pool_q.at[1])
    back_pool = fetch(pool.at[:, q_cols(xb)], pool_q.at[2])
    own_pool = fetch(pool.at[:, q_cols(x)], pool_q.at[3])

    local_ids = ids[...] - device_index * pool_rows
    row_ids = lax.broadcasted_iota(jnp.int32, (pool_rows, tokens), 0)
    chosen = jnp.where(row_ids == local_ids, 1.0, 0.0).astype(F32).T.astype(BF16)

    def pick(index, target, row_slot):
        def step(n, carry):
            cols = pl.ds(pl.multiple_of(n * tile, tile), tile)
            target[row_slot, cols] = dot_nn(chosen, pool_q[index, :, cols]).astype(BF16)
            return carry

        lax.fori_loop(0, quarter // tile, step, 0)

    every = pl.ds(0, tokens)
    far_pool.wait()
    pick(0, picked.at[0], every)
    x_via = wire.send(picked.at[0], via_x, x_next)
    c_next = wire.send(cot.at[:, q_cols(xn)], tok_c.at[slot(x, core), :], x_next)

    w_pair.wait()
    w_down.wait()
    wx_pair.wait_recv()
    wx_down.wait_recv()

    def w_block(zz, rows, cols):
        return weights.at[zz, all_p, rows, cols]

    def same(view, device_):
        return wire.send(view, view, device_)

    a_next = same(w_block(z, rows_of(y), cols_a), y_next)
    a_back = same(w_block(z, rows_of(y), cols_a), y_back)
    b_next = same(w_block(z, rows_of(y), cols_b), z_next)
    b_back = same(w_block(z, rows_of(y), cols_b), z_back)

    own_pool.wait()
    pick(3, tok_x, slot(x, core))
    dd_own_x = same(tok_x.at[slot(x, core), :], partner)
    c_own.wait()
    dd_own_c = same(tok_c.at[slot(x, core), :], partner)
    next_pool.wait()
    pick(1, picked.at[1], every)
    back_pool.wait()
    pick(2, picked.at[2], every)

    a_next.wait_recv()
    a_on = same(w_block(z, low_rows_of(yb), cols_a), y_next)
    a_back.wait_recv()
    a_off = same(w_block(z, high_rows_of(yn), cols_a), y_back)
    b_next.wait_recv()
    b_on = same(w_block(zb, low_rows_of(y), cols_b), z_next)
    b_back.wait_recv()
    b_off = same(w_block(zn, high_rows_of(y), cols_b), z_back)

    a_on.wait_recv()
    a_off.wait_recv()
    every_row = pl.ds(0, chunk_rows)
    lower, upper = pl.ds(0, chunk_rows // 2), pl.ds(chunk_rows // 2, chunk_rows // 2)
    a2_next = same(w_block(z, every_row, cols_a), z_next)
    a2_back = same(w_block(z, every_row, cols_a), z_back)
    b_on.wait_recv()
    b_off.wait_recv()
    b2_next = same(w_block(pl.ds(0, 4), rows_of(y), cols_b), y_next)
    b2_back = same(w_block(pl.ds(0, 4), rows_of(y), cols_b), y_back)

    c_via.wait_recv()
    c_pass = wire.send(via_c, tok_c.at[slot(xn, core), :], x_back)
    x_back_copy = wire.send(picked.at[2], tok_x.at[slot(x, core), :], x_back)
    x_via.wait_recv()
    x_pass = wire.send(via_x, tok_x.at[slot(xb, core), :], x_next)
    x_next_copy = wire.send(picked.at[1], tok_x.at[slot(x, core), :], x_next)

    c_back.wait_recv()
    dd_c_n = same(tok_c.at[slot(xn, core), :], partner)
    c_next.wait_recv()
    dd_c_b = same(tok_c.at[slot(xb, core), :], partner)

    a2_next.wait_recv()
    a2_on = same(w_block(zb, lower, cols_a), z_next)
    a2_back.wait_recv()
    a2_off = same(w_block(zn, upper, cols_a), z_back)
    b2_next.wait_recv()
    b2_on = same(w_block(pl.ds(0, 2), rows_of(yb), cols_b), y_next)
    b2_back.wait_recv()
    b2_off = same(w_block(pl.ds(2, 2), rows_of(yn), cols_b), y_back)

    c_pass.wait_recv()
    dd_c_f = same(tok_c.at[slot(xf, core), :], partner)
    x_pass.wait_recv()
    dd_x_f = same(tok_x.at[slot(xf, core), :], partner)

    for copy in (a2_on, a2_off, b2_on, b2_off):
        copy.wait_recv()

    def forward(xx, target):
        def step(j, carry):
            tx = tok_x[chip_slot(xx), :]
            for h in range(2):
                pair = weights[2 * j + h, 0:2].reshape(2 * chunk_rows, quarter)
                target[2 * j + h, :, 0 : 2 * chunk_rows] = dot_nt(tx, pair).astype(target.dtype)
            tc = tok_c[chip_slot(xx), :]
            both = weights[pl.ds(2 * j, 2), 2].reshape(2 * chunk_rows, quarter)
            back = dot_nt(tc, both).astype(target.dtype)
            target[2 * j, :, 2 * chunk_rows :] = back[:, :chunk_rows]
            target[2 * j + 1, :, 2 * chunk_rows :] = back[:, chunk_rows:]
            return carry

        lax.fori_loop(0, 2, step, 0)

    first, second = pl.ds(0, tokens), pl.ds(tokens, tokens)
    dd_c_f.wait_recv()
    dd_x_f.wait_recv()
    forward(xf, part.at[xf])
    order = (zf, zn, zb, z)
    rs1 = []
    for zz in order:
        rs1.append(
            (
                wire.send(part.at[xf, zz, first, :], r1p.at[zz], x_next),
                wire.send(part.at[xf, zz, second, :], r1m.at[zz], x_back),
            )
        )
    dd_own_x.wait_recv()
    dd_own_c.wait_recv()
    forward(x, part_own)

    x_back_copy.wait_recv()
    dd_x_n = same(tok_x.at[slot(xn, core), :], partner)
    x_next_copy.wait_recv()
    dd_x_b = same(tok_x.at[slot(xb, core), :], partner)
    dd_c_n.wait_recv()
    dd_x_n.wait_recv()
    forward(xn, part.at[xn])
    dd_c_b.wait_recv()
    dd_x_b.wait_recv()
    forward(xb, part.at[xb])

    def add_into(ref, *others):
        total = ref[...].astype(F32)
        for other in others:
            total = total + other[...].astype(F32)
        ref[...] = total.astype(ref.dtype)

    rs2 = []
    for k, zz in enumerate(order):
        rs1[k][0].wait_recv()
        add_into(part.at[xn, zz, first, :], r1p.at[zz])
        fwd = wire.send(part.at[xn, zz], r2p.at[zz], x_next)
        rs1[k][1].wait_recv()
        add_into(part.at[xb, zz, second, :], r1m.at[zz])
        rs2.append((fwd, wire.send(part.at[xb, zz], r2m.at[zz], x_back)))

    level = exponent[0]
    unscale = jnp.float32(0.0)
    for power in range(16):
        unscale = jnp.where(level == power, jnp.float32(0.5**power), unscale)

    def own_lanes(xx):
        return pl.ds(pl.multiple_of(xx * chip_tokens, chip_tokens), chip_tokens)

    def low_lanes(xx):
        return pl.ds(pl.multiple_of(xx * chip_tokens, tokens), tokens)

    def high_lanes(xx):
        return pl.ds(pl.multiple_of(xx * chip_tokens + tokens, tokens), tokens)

    every_unit = pl.ds(0, chunk_rows)
    ag = []
    for k, zz in enumerate(order):
        rs2[k][0].wait_recv()
        rs2[k][1].wait_recv()
        total = part_own[zz] + r2p[zz].astype(F32) + r2m[zz].astype(F32)
        gate = total[:, :chunk_rows]
        up = total[:, chunk_rows : 2 * chunk_rows]
        delta = unscale * total[:, 2 * chunk_rows :]
        sig = 1.0 / (1.0 + jnp.exp(-gate))
        hidden = gate * sig * up
        delta_gate = delta * up * sig * (1.0 + gate * (1.0 - sig))
        delta_up = delta * gate * sig
        deltas[zz, 0, :, own_lanes(x)] = delta_gate.T.astype(BF16)
        deltas[zz, 1, :, own_lanes(x)] = delta_up.T.astype(BF16)
        deltas[zz, 2, :, own_lanes(x)] = hidden.T.astype(BF16)
        mine = deltas.at[zz, all_p, every_unit, own_lanes(x)]
        ag.append((same(mine, x_next), same(mine, x_back)))

    passed = []

    def pass_on(k):
        zz = order[k]
        ag[k][0].wait_recv()
        on = same(deltas.at[zz, all_p, every_unit, low_lanes(xb)], x_next)
        ag[k][1].wait_recv()
        passed.append((on, same(deltas.at[zz, all_p, every_unit, high_lanes(xn)], x_back)))

    def gradient(k):
        zz = order[k]
        passed[k][0].wait_recv()
        passed[k][1].wait_recv()

        def step(n, carry):
            cols = pl.ds(pl.multiple_of(n * tile, tile), tile)
            pair = deltas[zz, 0:2].reshape(2 * chunk_rows, 4 * chip_tokens)
            out = dot_nn(pair, tok_x[:, cols]).astype(BF16)
            grads[zz, 0, :, cols] = out[:chunk_rows]
            grads[zz, 1, :, cols] = out[chunk_rows:]
            down_part = unscale * dot_nn(deltas[zz, 2], tok_c[:, cols])
            grads[zz, 2, :, cols] = down_part.astype(BF16)
            return carry

        lax.fori_loop(0, quarter // tile, step, 0)

    def g_block(zz, rows, cols):
        return grads.at[zz, all_p, rows, cols]

    def add3(out, *terms):
        for p in range(3):
            total = terms[0][p].astype(F32)
            for term in terms[1:]:
                total = total + term[p].astype(F32)
            out[p] = total.astype(out.dtype)

    yb1, yb2 = {}, {}

    def b_first(k):
        zz = order[k]
        yb1[k] = (
            wire.send(g_block(zz, low_rows_of(yf), cols_b), yb1p.at[zz], y_next),
            wire.send(g_block(zz, high_rows_of(yf), cols_b), yb1m.at[zz], y_back),
        )

    def b_second(k):
        zz = order[k]
        yb1[k][0].wait_recv()
        view = g_block(zz, low_rows_of(yn), cols_b)
        add3(view, view, yb1p.at[zz])
        on = wire.send(g_block(zz, rows_of(yn), cols_b), yb2p.at[zz], y_next)
        yb1[k][1].wait_recv()
        view = g_block(zz, high_rows_of(yb), cols_b)
        add3(view, view, yb1m.at[zz])
        yb2[k] = (on, wire.send(g_block(zz, rows_of(yb), cols_b), yb2m.at[zz], y_back))

    def b_sum(k, *more):
        zz = order[k]
        yb2[k][0].wait_recv()
        yb2[k][1].wait_recv()
        add3(sum_b.at[zz], g_block(zz, rows_of(y), cols_b), yb2p.at[zz], yb2m.at[zz])

    own_low, own_high = pl.ds(0, own_rows), pl.ds(own_rows, own_rows)

    def s_block(zz, rows):
        return sum_b.at[zz, all_p, rows, :]

    pass_on(0)
    pass_on(1)
    gradient(0)
    za1 = (
        wire.send(g_block(zf, lower, cols_a), ra1p, z_next),
        wire.send(g_block(zf, upper, cols_a), ra1m, z_back),
    )
    b_first(0)
    pass_on(2)

    gradient(1)
    za1[0].wait_recv()
    view = g_block(zn, lower, cols_a)
    add3(view, view, ra1p)
    za2_next = wire.send(g_block(zn, every_row, cols_a), ra2p, z_next)
    b_first(1)
    b_second(0)
    pass_on(3)

    gradient(2)
    za1[1].wait_recv()
    view = g_block(zb, upper, cols_a)
    add3(view, view, ra1m)
    za2_back = wire.send(g_block(zb, every_row, cols_a), ra2m, z_back)
    b_first(2)
    b_second(1)
    b_sum(0)
    zb1 = (
        wire.send(s_block(zf, own_low), zb1p, z_next),
        wire.send(s_block(zf, own_high), zb1m, z_back),
    )

    gradient(3)
    b_first(3)
    za2_next.wait_recv()
    za2_back.wait_recv()
    add3(sum_a, g_block(z, every_row, cols_a), ra2p, ra2m)

    def a_block(rows):
        return sum_a.at[all_p, rows, :]

    ya1 = (
        wire.send(a_block(low_rows_of(yf)), ya1p, y_next),
        wire.send(a_block(high_rows_of(yf)), ya1m, y_back),
    )
    b_second(2)
    b_sum(1)
    zb1[0].wait_recv()
    view = s_block(zn, own_low)
    add3(view, view, zb1p)
    zb2_next = wire.send(sum_b.at[zn], zb2p, z_next)
    b_second(3)
    ya1[0].wait_recv()
    view = a_block(low_rows_of(yn))
    add3(view, view, ya1p)
    ya2_next = wire.send(a_block(rows_of(yn)), ya2p, y_next)
    ya1[1].wait_recv()
    view = a_block(high_rows_of(yb))
    add3(view, view, ya1m)
    ya2_back = wire.send(a_block(rows_of(yb)), ya2m, y_back)
    b_sum(2)
    zb1[1].wait_recv()
    view = s_block(zb, own_high)
    add3(view, view, zb1m)
    zb2_back = wire.send(sum_b.at[zb], zb2m, z_back)
    b_sum(3)
    ya2_next.wait_recv()
    ya2_back.wait_recv()
    add3(final.at[all_p, pl.ds(0, pair_rows), cols_a], a_block(rows_of(y)), ya2p, ya2m)
    zb2_next.wait_recv()
    zb2_back.wait_recv()
    add3(final.at[all_p, pl.ds(0, pair_rows), cols_b], sum_b.at[z], zb2p, zb2m)

    kept = pl.ds(pl.multiple_of(x_hi * own_rows, own_rows), own_rows)
    given = pl.ds(pl.multiple_of((1 - x_hi) * own_rows, own_rows), own_rows)
    last = wire.send(final.at[all_p, given, :], crossed, x_far)
    out_pair[:, :, x_hi_cols] = final[0:2, kept, :]
    out_down[:, x_hi_cols] = final[2, kept, :]
    last.wait_recv()
    out_pair[:, :, other_cols] = crossed[0:2]
    out_down[:, other_cols] = crossed[2]
    wire.drain()


def per_device(x_pool, token_ids, cotangent, gate_up, down_weight, loss_exponent):
    tokens, width = cotangent.shape
    quarter = width // 4
    half = quarter // 2
    own_rows = down_weight.shape[0]
    pair_rows, chunk_rows = 2 * own_rows, 8 * own_rows
    chip_tokens, ring_tokens = 2 * tokens, 8 * tokens
    acts = 3 * chunk_rows

    def held(*shape, dtype=BF16):
        return pltpu.VMEM(shape, dtype)

    scratch = [
        held(ring_tokens, quarter), held(ring_tokens, quarter),
        held(tokens, quarter), held(tokens, quarter),
        held(3, tokens, quarter), held(4, x_pool.shape[0], quarter),
        held(4, 3, chunk_rows, quarter),
        held(4, 4, chip_tokens, acts), held(4, chip_tokens, acts, dtype=F32),
        held(4, tokens, acts), held(4, tokens, acts),
        held(4, chip_tokens, acts), held(4, chip_tokens, acts),
        held(4, 3, chunk_rows, ring_tokens),
        held(4, 3, chunk_rows, quarter),
        held(3, chunk_rows // 2, half), held(3, chunk_rows // 2, half),
        held(3, chunk_rows, half), held(3, chunk_rows, half),
        held(3, chunk_rows, half),
        held(3, own_rows, half), held(3, own_rows, half),
        held(3, pair_rows, half), held(3, pair_rows, half),
        held(4, 3, own_rows, half), held(4, 3, own_rows, half),
        held(4, 3, pair_rows, half), held(4, 3, pair_rows, half),
        held(4, 3, pair_rows, half),
        held(3, own_rows, half), held(3, own_rows, half),
        held(3, pair_rows, half), held(3, pair_rows, half),
        held(3, pair_rows, quarter), held(3, own_rows, quarter),
        pltpu.SemaphoreType.DMA((COPIES,)),
        pltpu.SemaphoreType.DMA((COPIES,)),
        pltpu.SemaphoreType.DMA((LOCALS,)),
    ]
    far = pl.BlockSpec(memory_space=pl.ANY)
    near = pl.BlockSpec(memory_space=pltpu.VMEM)
    return pl.pallas_call(
        kernel,
        out_shape=(
            jax.ShapeDtypeStruct(gate_up.shape, BF16),
            jax.ShapeDtypeStruct(down_weight.shape, BF16),
        ),
        in_specs=[far, near, far, far, far, pl.BlockSpec(memory_space=pltpu.SMEM)],
        out_specs=(near, near),
        scratch_shapes=scratch,
        compiler_params=pltpu.CompilerParams(
            collective_id=0, has_side_effects=True, vmem_limit_bytes=64_000_000
        ),
    )(x_pool, token_ids.reshape(1, tokens), cotangent, gate_up, down_weight, loss_exponent)


def solution(mesh):
    in_specs = (
        P(("grp", "wide"), None),
        P(("grp", "wide")),
        P(("grp", "wide"), None),
        P(None, "wide", "grp"),
        P("wide", "grp"),
        P(),
    )
    out_specs = (P(None, "wide", "grp"), P("wide", "grp"))
    return jax.shard_map(
        per_device, mesh=mesh, in_specs=in_specs, out_specs=out_specs, check_vma=False
    )
```

time: 771 us -> 156 us (0.20)
  waiting for transfers between devices: 603 us -> 0 us
  Pallas kernels: 0 us -> 149 us
  other arithmetic: 65.6 us -> 0 us
  matrix products: 41.8 us -> 0 us
  blocking collectives: 23.1 us -> 0 us
  starting transfers between devices: 19.1 us -> 0 us
  local copies, waits for them, and re-layouts: 16 us -> 3.19 us
    ppermute x9 -> x0, waiting for transfers between devices: 603 us -> none  [swapped(): return lax.ppermute(value, axis, pairs)]
    pallas_call x0 -> x1, Pallas kernels: none -> 149 us  [per_device(): pl.pallas_call(kernel, out_shape=(jax.ShapeDtypeStruct(gate_up.shape, BF1...]
    dot_general x4 -> x0, matrix products: 41.8 us -> none  [the longest x2 21.9 us: contract_first(): lax.dot_general(left_side, right_side, (((0,), (0,)), ((), ())), preferre...]
    concatenate x5 -> x0, other arithmetic: 37.8 us -> none  [the longest x3 28.1 us: per_device(): gathered = jnp.concatenate([gathered, partner_tokens], axis=1)]
    all_to_all x2 -> x0, blocking collectives: 23.1 us -> none  [the longest x1 12.7 us: summed_on_arrival(): parts = lax.all_to_all(split_up(x, dim, devices), axis, 0, 0, tiled=True)]
    ppermute x9 -> x0, starting transfers between devices: 19.1 us -> none  [swapped(): return lax.ppermute(value, axis, pairs)]
    select_n x4 -> x0, other arithmetic: 13.4 us -> none  [the longest x3 11.5 us: per_device(): jnp.where(own_bit == 0, jnp.concatenate([weight_rows, partner], axis=1),...]
    gather x1 -> x0, local copies, waits for them, and re-layouts: 8.66 us -> none  [per_device(): picked = jnp.take(x_pool, local_rows, axis=0)]
  transfers between devices with their start and end apart: 9 -> 0, of which waited for: 9 -> 0; matrix products, arithmetic and copies ran while one was open for 2% -> 0% of each run, Pallas kernels for 0% -> 0%
where the time goes in v1:
time: 156 us; the launch traced here: 153 us
  Pallas kernels  149 us (96%)
  local copies, waits for them, and re-layouts  3.19 us (2%)
    pallas_call x1, Pallas kernels, per_device(): pl.pallas_call(kernel, out_shape=(jax.ShapeDtypeStruct(gate_up.shape, BF1...  149 us
    unnamed x2, local copies, waits for them, and re-layouts  3.19 us

profile of v1, /device:TPU:0, one launch (start us, length us, event | category | flops | bytes accessed | tf_op | source)
XLA Modules:
  0.0 153.3 jit_solution(9438477578928942190)
XLA Ops:
  1.3 148.8 %shard_map.77 = (bf16[2,16,3584]{2,1,0:T(8,128)(2,1)}, bf16[16,3584]{1,0:T(8,128)(2,1)}) custom-call(bf16[512,7168]{1,0:T(8,128)(2,1)} %pool.1, s32[1,128]{1,0:T(1,128)} %bitcast.1, bf16[128,7168]{1,0:T(8,128)(2,1)} %cot.1, bf16[2,16,3584]{2,1,0:T(8,128)(2,1)} %gate_up.1, bf16[16,3584]{1,0:T(8,128)(2,1)} %down.1, s32[1]{0:T(128)S(6)} %copy.10.exponent), custom_call_target="tpu_custom_call" | custom-call | tf_op jit(solution)/shard_map/pallas_call | solution.py:525
  150.1 1.6 %copy.11 = bf16[2,16,3584]{2,1,0:T(8,128)(2,1)} copy(bf16[2,16,3584]{2,1,0:T(8,128)(2,1)} %get-tuple-element.4) | data formatting | bytes 458752
  151.7 1.6 %copy.12 = bf16[16,3584]{1,0:T(8,128)(2,1)} copy(bf16[16,3584]{1,0:T(8,128)(2,1)} %get-tuple-element.5) | data formatting | bytes 229376

commit v2 on v1

--- a/solution.py
+++ b/solution.py
@@ -12,6 +12,7 @@
 F32 = jnp.float32
 COPIES = 128
 LOCALS = 16
+TILE = 256
 
 
 def dot_nt(a, b):
@@ -20,6 +21,12 @@
 
 def dot_nn(a, b):
     return lax.dot_general(a, b, (((1,), (0,)), ((), ())), preferred_element_type=F32)
+
+
+def split_columns(quarter):
+    tiles = quarter // TILE
+    low = max(1, 3 * tiles // 7)
+    return low * TILE, (tiles - low) * TILE
 
 
 class Wire:
@@ -52,8 +59,8 @@
     out_pair, out_down,
     tok_x, tok_c, via_x, via_c, picked, pool_q, weights,
     part, part_own, r1p, r1m, r2p, r2m, deltas, grads,
-    ra1p, ra1m, ra2p, ra2m, sum_a, ya1p, ya1m, ya2p, ya2m,
-    yb1p, yb1m, yb2p, yb2m, sum_b, zb1p, zb1m, zb2p, zb2m,
+    ring_a, sum_a, ya1p, ya1m, ya2p, ya2m,
+    yb1p, yb1m, yb2p, yb2m, sum_b, ring_b,
     final, crossed, send_sems, recv_sems, local_sems,
 ):
     tokens, width = cot.shape
@@ -64,7 +71,8 @@
     chunk_rows = 4 * pair_rows
     chip_tokens = 2 * tokens
     pool_rows = pool.shape[0]
-    tile = 256 if quarter % 256 == 0 else quarter
+    tile = TILE
+    part_a, part_b = split_columns(quarter)
 
     x_lo = lax.axis_index("grp")
     wide = lax.axis_index("wide")
@@ -84,9 +92,11 @@
     xn, xf, xb = shift(x, 1), shift(x, 2), shift(x, -1)
     yn, yf, yb = shift(y, 1), shift(y, 2), shift(y, -1)
     zn, zf, zb = shift(z, 1), shift(z, 2), shift(z, -1)
+    z_on, z_off = (lax.rem(z + 4 + s, 4) for s in (1 - 2 * core, 2 * core - 1))
     x_next, x_far, x_back = (device(v, y, z, core) for v in (xn, xf, xb))
     y_next, y_back = (device(x, v, z, core) for v in (yn, yb))
     z_next, z_back = (device(x, y, v, core) for v in (zn, zb))
+    z_ring = device(x, y, z_on, core)
     partner = device(x, y, z, 1 - core)
 
     def feature_quarter(xx):
@@ -260,7 +270,7 @@
     dd_c_f.wait_recv()
     dd_x_f.wait_recv()
     forward(xf, part.at[xf])
-    order = (zf, zn, zb, z)
+    order = (z_off, zf, z_on, z)
     rs1 = []
     for zz in order:
         rs1.append(
@@ -290,32 +300,34 @@
             total = total + other[...].astype(F32)
         ref[...] = total.astype(ref.dtype)
 
-    rs2 = []
-    for k, zz in enumerate(order):
+    def own_lanes(xx):
+        return pl.ds(pl.multiple_of(xx * chip_tokens, chip_tokens), chip_tokens)
+
+    def low_lanes(xx):
+        return pl.ds(pl.multiple_of(xx * chip_tokens, tokens), tokens)
+
+    def high_lanes(xx):
+        return pl.ds(pl.multiple_of(xx * chip_tokens + tokens, tokens), tokens)
+
+    level = exponent[0]
+    unscale = jnp.float32(0.0)
+    for power in range(16):
+        unscale = jnp.where(level == power, jnp.float32(0.5**power), unscale)
+
+    every_unit = pl.ds(0, chunk_rows)
+    rs2, ag, passed, yb1, yb2 = {}, {}, {}, {}, {}
+
+    def reduce_on(k):
+        zz = order[k]
         rs1[k][0].wait_recv()
         add_into(part.at[xn, zz, first, :], r1p.at[zz])
         fwd = wire.send(part.at[xn, zz], r2p.at[zz], x_next)
         rs1[k][1].wait_recv()
         add_into(part.at[xb, zz, second, :], r1m.at[zz])
-        rs2.append((fwd, wire.send(part.at[xb, zz], r2m.at[zz], x_back)))
-
-    level = exponent[0]
-    unscale = jnp.float32(0.0)
-    for power in range(16):
-        unscale = jnp.where(level == power, jnp.float32(0.5**power), unscale)
-
-    def own_lanes(xx):
-        return pl.ds(pl.multiple_of(xx * chip_tokens, chip_tokens), chip_tokens)
-
-    def low_lanes(xx):
-        return pl.ds(pl.multiple_of(xx * chip_tokens, tokens), tokens)
-
-    def high_lanes(xx):
-        return pl.ds(pl.multiple_of(xx * chip_tokens + tokens, tokens), tokens)
-
-    every_unit = pl.ds(0, chunk_rows)
-    ag = []
-    for k, zz in enumerate(order):
+        rs2[k] = (fwd, wire.send(part.at[xb, zz], r2m.at[zz], x_back))
+
+    def activate(k):
+        zz = order[k]
         rs2[k][0].wait_recv()
         rs2[k][1].wait_recv()
         total = part_own[zz] + r2p[zz].astype(F32) + r2m[zz].astype(F32)
@@ -329,25 +341,27 @@
         deltas[zz, 0, :, own_lanes(x)] = delta_gate.T.astype(BF16)
         deltas[zz, 1, :, own_lanes(x)] = delta_up.T.astype(BF16)
         deltas[zz, 2, :, own_lanes(x)] = hidden.T.astype(BF16)
-        mine = deltas.at[zz, all_p, every_unit, own_lanes(x)]
-        ag.append((same(mine, x_next), same(mine, x_back)))
-
-    passed = []
+
+    def gather(k):
+        mine = deltas.at[order[k], all_p, every_unit, own_lanes(x)]
+        ag[k] = (same(mine, x_next), same(mine, x_back))
 
     def pass_on(k):
         zz = order[k]
         ag[k][0].wait_recv()
         on = same(deltas.at[zz, all_p, every_unit, low_lanes(xb)], x_next)
         ag[k][1].wait_recv()
-        passed.append((on, same(deltas.at[zz, all_p, every_unit, high_lanes(xn)], x_back)))
-
-    def gradient(k):
-        zz = order[k]
+        passed[k] = (on, same(deltas.at[zz, all_p, every_unit, high_lanes(xn)], x_back))
+
+    def gathered(k):
         passed[k][0].wait_recv()
         passed[k][1].wait_recv()
 
+    def grad_half(k, start, size):
+        zz = order[k]
+
         def step(n, carry):
-            cols = pl.ds(pl.multiple_of(n * tile, tile), tile)
+            cols = pl.ds(pl.multiple_of(start + n * tile, tile), tile)
             pair = deltas[zz, 0:2].reshape(2 * chunk_rows, 4 * chip_tokens)
             out = dot_nn(pair, tok_x[:, cols]).astype(BF16)
             grads[zz, 0, :, cols] = out[:chunk_rows]
@@ -356,7 +370,9 @@
             grads[zz, 2, :, cols] = down_part.astype(BF16)
             return carry
 
-        lax.fori_loop(0, quarter // tile, step, 0)
+        lax.fori_loop(0, size // tile, step, 0)
+
+    cols_a, cols_b = pl.ds(0, part_a), pl.ds(part_a, part_b)
 
     def g_block(zz, rows, cols):
         return grads.at[zz, all_p, rows, cols]
@@ -368,7 +384,21 @@
                 total = total + term[p].astype(F32)
             out[p] = total.astype(out.dtype)
 
-    yb1, yb2 = {}, {}
+    ring_of_a, ring_of_b = [], []
+
+    def a_step(k):
+        view = g_block(order[k], every_row, cols_a)
+        if k > 0:
+            ring_of_a[k - 1].wait_recv()
+            add3(view, view, ring_a.at[k - 1])
+        ring_of_a.append(wire.send(view, ring_a.at[k], z_ring))
+
+    def b_step(k):
+        view = sum_b.at[order[k]]
+        if k > 0:
+            ring_of_b[k - 1].wait_recv()
+            add3(view, view, ring_b.at[k - 1])
+        ring_of_b.append(wire.send(view, ring_b.at[k], z_ring))
 
     def b_first(k):
         zz = order[k]
@@ -388,54 +418,61 @@
         add3(view, view, yb1m.at[zz])
         yb2[k] = (on, wire.send(g_block(zz, rows_of(yb), cols_b), yb2m.at[zz], y_back))
 
-    def b_sum(k, *more):
+    def b_sum(k):
         zz = order[k]
         yb2[k][0].wait_recv()
         yb2[k][1].wait_recv()
         add3(sum_b.at[zz], g_block(zz, rows_of(y), cols_b), yb2p.at[zz], yb2m.at[zz])
 
-    own_low, own_high = pl.ds(0, own_rows), pl.ds(own_rows, own_rows)
-
-    def s_block(zz, rows):
-        return sum_b.at[zz, all_p, rows, :]
-
+    reduce_on(0)
+    reduce_on(1)
+    activate(0)
+    gather(0)
+    reduce_on(2)
+    activate(1)
     pass_on(0)
+    gather(1)
+    reduce_on(3)
+    activate(2)
+
+    gathered(0)
+    grad_half(0, 0, part_a)
+    a_step(0)
+    grad_half(0, part_a, part_b)
+    b_first(0)
     pass_on(1)
-    gradient(0)
-    za1 = (
-        wire.send(g_block(zf, lower, cols_a), ra1p, z_next),
-        wire.send(g_block(zf, upper, cols_a), ra1m, z_back),
-    )
-    b_first(0)
+    gather(2)
+    b_second(0)
+    activate(3)
+    gather(3)
+
+    gathered(1)
+    grad_half(1, 0, part_a)
+    a_step(1)
+    grad_half(1, part_a, part_b)
+    b_first(1)
     pass_on(2)
-
-    gradient(1)
-    za1[0].wait_recv()
-    view = g_block(zn, lower, cols_a)
-    add3(view, view, ra1p)
-    za2_next = wire.send(g_block(zn, every_row, cols_a), ra2p, z_next)
-    b_first(1)
-    b_second(0)
+    b_sum(0)
+    b_step(0)
+    b_second(1)
     pass_on(3)
 
-    gradient(2)
-    za1[1].wait_recv()
-    view = g_block(zb, upper, cols_a)
-    add3(view, view, ra1m)
-    za2_back = wire.send(g_block(zb, every_row, cols_a), ra2m, z_back)
+    gathered(2)
+    grad_half(2, 0, part_a)
+    a_step(2)
+    grad_half(2, part_a, part_b)
     b_first(2)
-    b_second(1)
-    b_sum(0)
-    zb1 = (
-        wire.send(s_block(zf, own_low), zb1p, z_next),
-        wire.send(s_block(zf, own_high), zb1m, z_back),
-    )
-
-    gradient(3)
+    b_sum(1)
+    b_step(1)
+
+    gathered(3)
+    grad_half(3, part_a, part_b)
     b_first(3)
-    za2_next.wait_recv()
-    za2_back.wait_recv()
-    add3(sum_a, g_block(z, every_row, cols_a), ra2p, ra2m)
+    b_second(2)
+    grad_half(3, 0, part_a)
+    b_second(3)
+    ring_of_a[2].wait_recv()
+    add3(sum_a, g_block(z, every_row, cols_a), ring_a.at[2])
 
     def a_block(rows):
         return sum_a.at[all_p, rows, :]
@@ -444,13 +481,8 @@
         wire.send(a_block(low_rows_of(yf)), ya1p, y_next),
         wire.send(a_block(high_rows_of(yf)), ya1m, y_back),
     )
-    b_second(2)
-    b_sum(1)
-    zb1[0].wait_recv()
-    view = s_block(zn, own_low)
-    add3(view, view, zb1p)
-    zb2_next = wire.send(sum_b.at[zn], zb2p, z_next)
-    b_second(3)
+    b_sum(2)
+    b_step(2)
     ya1[0].wait_recv()
     view = a_block(low_rows_of(yn))
     add3(view, view, ya1p)
@@ -459,25 +491,26 @@
     view = a_block(high_rows_of(yb))
     add3(view, view, ya1m)
     ya2_back = wire.send(a_block(rows_of(yb)), ya2m, y_back)
-    b_sum(2)
-    zb1[1].wait_recv()
-    view = s_block(zb, own_high)
-    add3(view, view, zb1m)
-    zb2_back = wire.send(sum_b.at[zb], zb2m, z_back)
     b_sum(3)
+    ring_of_b[2].wait_recv()
+    every_pair = pl.ds(0, pair_rows)
+    add3(final.at[all_p, every_pair, cols_b], sum_b.at[z], ring_b.at[2])
+    kept = pl.ds(pl.multiple_of(x_hi * own_rows, own_rows), own_rows)
+    given = pl.ds(pl.multiple_of((1 - x_hi) * own_rows, own_rows), own_rows)
+    every_own = pl.ds(0, own_rows)
+    last_b = wire.send(
+        final.at[all_p, given, cols_b], crossed.at[all_p, every_own, cols_b], x_far
+    )
     ya2_next.wait_recv()
     ya2_back.wait_recv()
-    add3(final.at[all_p, pl.ds(0, pair_rows), cols_a], a_block(rows_of(y)), ya2p, ya2m)
-    zb2_next.wait_recv()
-    zb2_back.wait_recv()
-    add3(final.at[all_p, pl.ds(0, pair_rows), cols_b], sum_b.at[z], zb2p, zb2m)
-
-    kept = pl.ds(pl.multiple_of(x_hi * own_rows, own_rows), own_rows)
-    given = pl.ds(pl.multiple_of((1 - x_hi) * own_rows, own_rows), own_rows)
-    last = wire.send(final.at[all_p, given, :], crossed, x_far)
+    add3(final.at[all_p, every_pair, cols_a], a_block(rows_of(y)), ya2p, ya2m)
+    last_a = wire.send(
+        final.at[all_p, given, cols_a], crossed.at[all_p, every_own, cols_a], x_far
+    )
     out_pair[:, :, x_hi_cols] = final[0:2, kept, :]
     out_down[:, x_hi_cols] = final[2, kept, :]
-    last.wait_recv()
+    last_b.wait_recv()
+    last_a.wait_recv()
     out_pair[:, :, other_cols] = crossed[0:2]
     out_down[:, other_cols] = crossed[2]
     wire.drain()
@@ -491,6 +524,7 @@
     pair_rows, chunk_rows = 2 * own_rows, 8 * own_rows
     chip_tokens, ring_tokens = 2 * tokens, 8 * tokens
     acts = 3 * chunk_rows
+    part_a, part_b = split_columns(quarter)
 
     def held(*shape, dtype=BF16):
         return pltpu.VMEM(shape, dtype)
@@ -505,16 +539,12 @@
         held(4, chip_tokens, acts), held(4, chip_tokens, acts),
         held(4, 3, chunk_rows, ring_tokens),
         held(4, 3, chunk_rows, quarter),
-        held(3, chunk_rows // 2, half), held(3, chunk_rows // 2, half),
-        held(3, chunk_rows, half), held(3, chunk_rows, half),
-        held(3, chunk_rows, half),
-        held(3, own_rows, half), held(3, own_rows, half),
-        held(3, pair_rows, half), held(3, pair_rows, half),
-        held(4, 3, own_rows, half), held(4, 3, own_rows, half),
-        held(4, 3, pair_rows, half), held(4, 3, pair_rows, half),
-        held(4, 3, pair_rows, half),
-        held(3, own_rows, half), held(3, own_rows, half),
-        held(3, pair_rows, half), held(3, pair_rows, half),
+        held(3, 3, chunk_rows, part_a), held(3, chunk_rows, part_a),
+        held(3, own_rows, part_a), held(3, own_rows, part_a),
+        held(3, pair_rows, part_a), held(3, pair_rows, part_a),
+        held(4, 3, own_rows, part_b), held(4, 3, own_rows, part_b),
+        held(4, 3, pair_rows, part_b), held(4, 3, pair_rows, part_b),
+        held(4, 3, pair_rows, part_b), held(3, 3, pair_rows, part_b),
         held(3, pair_rows, quarter), held(3, own_rows, quarter),
         pltpu.SemaphoreType.DMA((COPIES,)),
         pltpu.SemaphoreType.DMA((COPIES,)),

time: 156 us -> 136 us (0.87); the launches traced: 153 us -> 136 us
  Pallas kernels: 149 us -> 132 us
    pallas_call x1, Pallas kernels: 149 us -> 132 us  [per_device(): pl.pallas_call(kernel, out_shape=(jax.ShapeDtypeStruct(gate_up.shape, BF1...]
where the time goes in v2:
time: 136 us
  Pallas kernels  132 us (97%)
  local copies, waits for them, and re-layouts  3.19 us (2%)
    pallas_call x1, Pallas kernels, per_device(): pl.pallas_call(kernel, out_shape=(jax.ShapeDtypeStruct(gate_up.shape, BF1...  132 us
    unnamed x2, local copies, waits for them, and re-layouts  3.19 us

profile of v2, /device:TPU:0, one launch (start us, length us, event | category | flops | bytes accessed | tf_op | source)
XLA Modules:
  0.0 136.3 jit_solution(5355822064789589708)
XLA Ops:
  1.3 131.8 %shard_map.77 = (bf16[2,16,3584]{2,1,0:T(8,128)(2,1)}, bf16[16,3584]{1,0:T(8,128)(2,1)}) custom-call(bf16[512,7168]{1,0:T(8,128)(2,1)} %pool.1, s32[1,128]{1,0:T(1,128)} %bitcast.1, bf16[128,7168]{1,0:T(8,128)(2,1)} %cot.1, bf16[2,16,3584]{2,1,0:T(8,128)(2,1)} %gate_up.1, bf16[16,3584]{1,0:T(8,128)(2,1)} %down.1, s32[1]{0:T(128)S(6)} %copy.10.exponent), custom_call_target="tpu_custom_call" | custom-call | tf_op jit(solution)/shard_map/pallas_call | solution.py:555
  133.1 1.6 %copy.11 = bf16[2,16,3584]{2,1,0:T(8,128)(2,1)} copy(bf16[2,16,3584]{2,1,0:T(8,128)(2,1)} %get-tuple-element.4) | data formatting | bytes 458752
  134.7 1.6 %copy.12 = bf16[16,3584]{1,0:T(8,128)(2,1)} copy(bf16[16,3584]{1,0:T(8,128)(2,1)} %get-tuple-element.5) | data formatting | bytes 229376

commit v3 on v2

--- a/solution.py
+++ b/solution.py
@@ -61,7 +61,7 @@
     part, part_own, r1p, r1m, r2p, r2m, deltas, grads,
     ring_a, sum_a, ya1p, ya1m, ya2p, ya2m,
     yb1p, yb1m, yb2p, yb2m, sum_b, ring_b,
-    final, crossed, send_sems, recv_sems, local_sems,
+    final, crossed, ids_v, send_sems, recv_sems, local_sems,
 ):
     tokens, width = cot.shape
     quarter = width // 4
@@ -135,6 +135,7 @@
         copy.start()
         return copy
 
+    ids_here = fetch(ids, ids_v)
     far_pool = fetch(pool.at[:, q_cols(xf)], pool_q.at[0])
 
     barrier = pltpu.get_barrier_semaphore()
@@ -158,7 +159,8 @@
     back_pool = fetch(pool.at[:, q_cols(xb)], pool_q.at[2])
     own_pool = fetch(pool.at[:, q_cols(x)], pool_q.at[3])
 
-    local_ids = ids[...] - device_index * pool_rows
+    ids_here.wait()
+    local_ids = ids_v[...] - device_index * pool_rows
     row_ids = lax.broadcasted_iota(jnp.int32, (pool_rows, tokens), 0)
     chosen = jnp.where(row_ids == local_ids, 1.0, 0.0).astype(F32).T.astype(BF16)
 
@@ -343,17 +345,22 @@
         deltas[zz, 2, :, own_lanes(x)] = hidden.T.astype(BF16)
 
     def gather(k):
-        mine = deltas.at[order[k], all_p, every_unit, own_lanes(x)]
-        ag[k] = (same(mine, x_next), same(mine, x_back))
+        zz = order[k]
+        low = deltas.at[zz, all_p, every_unit, low_lanes(x)]
+        high = deltas.at[zz, all_p, every_unit, high_lanes(x)]
+        early = (same(low, x_next), same(high, x_back))
+        ag[k] = (early, (same(high, x_next), same(low, x_back)))
 
     def pass_on(k):
         zz = order[k]
-        ag[k][0].wait_recv()
+        ag[k][0][0].wait_recv()
         on = same(deltas.at[zz, all_p, every_unit, low_lanes(xb)], x_next)
-        ag[k][1].wait_recv()
+        ag[k][0][1].wait_recv()
         passed[k] = (on, same(deltas.at[zz, all_p, every_unit, high_lanes(xn)], x_back))
 
     def gathered(k):
+        ag[k][1][0].wait_recv()
+        ag[k][1][1].wait_recv()
         passed[k][0].wait_recv()
         passed[k][1].wait_recv()
 
@@ -438,39 +445,38 @@
     gathered(0)
     grad_half(0, 0, part_a)
     a_step(0)
+    pass_on(1)
+    gather(2)
     grad_half(0, part_a, part_b)
     b_first(0)
-    pass_on(1)
-    gather(2)
     b_second(0)
     activate(3)
-    gather(3)
 
     gathered(1)
     grad_half(1, 0, part_a)
     a_step(1)
+    pass_on(2)
+    gather(3)
     grad_half(1, part_a, part_b)
     b_first(1)
-    pass_on(2)
     b_sum(0)
     b_step(0)
+
+    gathered(2)
+    grad_half(2, 0, part_a)
     b_second(1)
     pass_on(3)
-
-    gathered(2)
-    grad_half(2, 0, part_a)
-    a_step(2)
     grad_half(2, part_a, part_b)
     b_first(2)
-    b_sum(1)
-    b_step(1)
+    a_step(2)
 
     gathered(3)
     grad_half(3, part_a, part_b)
     b_first(3)
     b_second(2)
+    b_sum(1)
+    b_step(1)
     grad_half(3, 0, part_a)
-    b_second(3)
     ring_of_a[2].wait_recv()
     add3(sum_a, g_block(z, every_row, cols_a), ring_a.at[2])
 
@@ -481,6 +487,7 @@
         wire.send(a_block(low_rows_of(yf)), ya1p, y_next),
         wire.send(a_block(high_rows_of(yf)), ya1m, y_back),
     )
+    b_second(3)
     b_sum(2)
     b_step(2)
     ya1[0].wait_recv()
@@ -546,11 +553,12 @@
         held(4, 3, pair_rows, part_b), held(4, 3, pair_rows, part_b),
         held(4, 3, pair_rows, part_b), held(3, 3, pair_rows, part_b),
         held(3, pair_rows, quarter), held(3, own_rows, quarter),
+        pltpu.VMEM((1, tokens), jnp.int32),
         pltpu.SemaphoreType.DMA((COPIES,)),
         pltpu.SemaphoreType.DMA((COPIES,)),
         pltpu.SemaphoreType.DMA((LOCALS,)),
     ]
-    far = pl.BlockSpec(memory_space=pl.ANY)
+    far = pl.BlockSpec(memory_space=pltpu.HBM)
     near = pl.BlockSpec(memory_space=pltpu.VMEM)
     return pl.pallas_call(
         kernel,
@@ -558,11 +566,11 @@
             jax.ShapeDtypeStruct(gate_up.shape, BF16),
             jax.ShapeDtypeStruct(down_weight.shape, BF16),
         ),
-        in_specs=[far, near, far, far, far, pl.BlockSpec(memory_space=pltpu.SMEM)],
+        in_specs=[far, far, far, far, far, pl.BlockSpec(memory_space=pltpu.SMEM)],
         out_specs=(near, near),
         scratch_shapes=scratch,
         compiler_params=pltpu.CompilerParams(
-            collective_id=0, has_side_effects=True, vmem_limit_bytes=64_000_000
+            collective_id=0, has_side_effects=True, vmem_limit_bytes=56_000_000
         ),
     )(x_pool, token_ids.reshape(1, tokens), cotangent, gate_up, down_weight, loss_exponent)
 

time: 136 us -> 132 us (0.971)
  Pallas kernels: 132 us -> 128 us
    pallas_call x1, Pallas kernels: 132 us -> 128 us  [per_device(): pl.pallas_call(kernel, out_shape=(jax.ShapeDtypeStruct(gate_up.shape, BF1...]
    unnamed x2 -> x6, local copies, waits for them, and re-layouts: 3.19 us -> 2.88 us
where the time goes in v3:
time: 132 us
  Pallas kernels  128 us (97%)
  local copies, waits for them, and re-layouts  2.88 us (2%)
    pallas_call x1, Pallas kernels, per_device(): pl.pallas_call(kernel, out_shape=(jax.ShapeDtypeStruct(gate_up.shape, BF1...  128 us
    unnamed x6, local copies, waits for them, and re-layouts  2.88 us

profile of v3, /device:TPU:0, one launch (start us, length us, event | category | flops | bytes accessed | tf_op | source)
XLA Modules:
  0.0 131.8 jit_solution(417957881367537013)
XLA Ops:
  1.3 0.0 copy-start
  1.3 0.9 copy-done
  2.2 0.0 copy-start.1
  2.2 0.7 copy-done.1
  2.8 127.6 %shard_map.77 = (bf16[2,16,3584]{2,1,0:T(8,128)(2,1)S(1)}, bf16[16,3584]{1,0:T(8,128)(2,1)S(1)}) custom-call(bf16[512,7168]{1,0:T(8,128)(2,1)} %pool.1, s32[1,128]{1,0:T(1,128)S(1)} %bitcast.1, bf16[128,7168]{1,0:T(8,128)(2,1)} %cot.1, bf16[2,16,3584]{2,1,0:T(8,128)(2,1)} %gate_up.1, bf16[16,3584]{1,0:T(8,128)(2,1)S(1)} %copy-done, s32[1]{0:T(128)S(6)} %copy.10.exponent), custom_call_target="tpu_custom_call" | custom-call | tf_op jit(solution)/shard_map/pallas_call | solution.py:563
  130.5 0.7 copy.11
  131.1 0.6 copy.12
Async XLA Ops:
  1.3 0.9 copy-start
  2.2 0.7 copy-start.1

commit v4 on v3

--- a/solution.py
+++ b/solution.py
@@ -10,8 +10,9 @@
 MESH = pl.DeviceIdType.MESH
 BF16 = jnp.bfloat16
 F32 = jnp.float32
-COPIES = 128
-LOCALS = 16
+COPIES = 103
+SENDS = 24
+LOCALS = 8
 TILE = 256
 
 
@@ -36,10 +37,13 @@
         self.sent = []
 
     def send(self, src, dst, device):
+        lane = self.count % SENDS
+        if self.count >= SENDS:
+            self.sent[self.count - SENDS].wait_send()
         copy = pltpu.make_async_remote_copy(
             src_ref=src,
             dst_ref=dst,
-            send_sem=self.send_sems.at[self.count],
+            send_sem=self.send_sems.at[lane],
             recv_sem=self.recv_sems.at[self.count],
             device_id=device,
             device_id_type=MESH,
@@ -50,7 +54,7 @@
         return copy
 
     def drain(self):
-        for copy in self.sent:
+        for copy in self.sent[-SENDS:]:
             copy.wait_send()
 
 
@@ -153,6 +157,13 @@
     w_down = fetch(down.at[:, x_hi_cols], weights.at[z, 2, owner_rows(x_hi), :])
 
     c_via = wire.send(cot.at[:, q_cols(xf)], via_c, x_back)
+    early, late = pl.ds(0, tokens // 2), pl.ds(tokens // 2, tokens // 2)
+
+    def half_slot(part_index):
+        start = (2 * x + core) * tokens + part_index * (tokens // 2)
+        return pl.ds(pl.multiple_of(start, tokens // 2), tokens // 2)
+
+    c_next_a = wire.send(cot.at[early, q_cols(xn)], tok_c.at[half_slot(0), :], x_next)
     c_back = wire.send(cot.at[:, q_cols(xb)], tok_c.at[slot(x, core), :], x_back)
     c_own = fetch(cot.at[:, q_cols(x)], tok_c.at[slot(x, core), :])
     next_pool = fetch(pool.at[:, q_cols(xn)], pool_q.at[1])
@@ -176,7 +187,7 @@
     far_pool.wait()
     pick(0, picked.at[0], every)
     x_via = wire.send(picked.at[0], via_x, x_next)
-    c_next = wire.send(cot.at[:, q_cols(xn)], tok_c.at[slot(x, core), :], x_next)
+    c_next_b = wire.send(cot.at[late, q_cols(xn)], tok_c.at[half_slot(1), :], x_next)
 
     w_pair.wait()
     w_down.wait()
@@ -233,7 +244,8 @@
 
     c_back.wait_recv()
     dd_c_n = same(tok_c.at[slot(xn, core), :], partner)
-    c_next.wait_recv()
+    c_next_a.wait_recv()
+    c_next_b.wait_recv()
     dd_c_b = same(tok_c.at[slot(xb, core), :], partner)
 
     a2_next.wait_recv()
@@ -554,7 +566,7 @@
         held(4, 3, pair_rows, part_b), held(3, 3, pair_rows, part_b),
         held(3, pair_rows, quarter), held(3, own_rows, quarter),
         pltpu.VMEM((1, tokens), jnp.int32),
-        pltpu.SemaphoreType.DMA((COPIES,)),
+        pltpu.SemaphoreType.DMA((SENDS,)),
         pltpu.SemaphoreType.DMA((COPIES,)),
         pltpu.SemaphoreType.DMA((LOCALS,)),
     ]

time: 132 us -> 130 us (0.985)
  Pallas kernels: 128 us -> 126 us
    pallas_call x1, Pallas kernels: 128 us -> 126 us  [per_device(): pl.pallas_call(kernel, out_shape=(jax.ShapeDtypeStruct(gate_up.shape, BF1...]
where the time goes in v4:
time: 130 us
  Pallas kernels  126 us (97%)
  local copies, waits for them, and re-layouts  2.88 us (2%)
  between operations  1.3 us (1%)
    pallas_call x1, Pallas kernels, per_device(): pl.pallas_call(kernel, out_shape=(jax.ShapeDtypeStruct(gate_up.shape, BF1...  126 us
    unnamed x6, local copies, waits for them, and re-layouts  2.88 us

profile of v4, /device:TPU:0, one launch (start us, length us, event | category | flops | bytes accessed | tf_op | source)
XLA Modules:
  0.0 130.3 jit_solution(1350624623345932004)
XLA Ops:
  1.3 0.0 copy-start
  1.3 0.9 copy-done
  2.2 0.0 copy-start.1
  2.2 0.7 copy-done.1
  2.8 126.1 %shard_map.77 = (bf16[2,16,3584]{2,1,0:T(8,128)(2,1)S(1)}, bf16[16,3584]{1,0:T(8,128)(2,1)S(1)}) custom-call(bf16[512,7168]{1,0:T(8,128)(2,1)} %pool.1, s32[1,128]{1,0:T(1,128)S(1)} %bitcast.1, bf16[128,7168]{1,0:T(8,128)(2,1)} %cot.1, bf16[2,16,3584]{2,1,0:T(8,128)(2,1)} %gate_up.1, bf16[16,3584]{1,0:T(8,128)(2,1)S(1)} %copy-done, s32[1]{0:T(128)S(6)} %copy.10.exponent), custom_call_target="tpu_custom_call" | custom-call | tf_op jit(solution)/shard_map/pallas_call | solution.py:575
  129.0 0.7 copy.11
  129.7 0.6 copy.12
Async XLA Ops:
  1.3 0.9 copy-start
  2.2 0.7 copy-start.1

commit v5 on v4

--- a/solution.py
+++ b/solution.py
@@ -584,7 +584,7 @@
         compiler_params=pltpu.CompilerParams(
             collective_id=0, has_side_effects=True, vmem_limit_bytes=56_000_000
         ),
-    )(x_pool, token_ids.reshape(1, tokens), cotangent, gate_up, down_weight, loss_exponent)
+    )(*[pltpu.with_memory_space_constraint(v, pltpu.HBM) for v in (x_pool, token_ids.reshape(1, tokens), cotangent, gate_up, down_weight)], loss_exponent)
 
 
 def solution(mesh):

time: 130 us -> 129 us (level)
  local copies, waits for them, and re-layouts: 2.88 us -> 1.34 us
    unnamed x6 -> x2, local copies, waits for them, and re-layouts: 2.88 us -> 1.34 us
where the time goes in v5:
time: 129 us
  Pallas kernels  126 us (98%)
  local copies, waits for them, and re-layouts  1.34 us (1%)
  between operations  1.29 us (1%)
    pallas_call x1, Pallas kernels, per_device(): pl.pallas_call(kernel, out_shape=(jax.ShapeDtypeStruct(gate_up.shape, BF1...  126 us

profile of v5, /device:TPU:0, one launch (start us, length us, event | category | flops | bytes accessed | tf_op | source)
XLA Modules:
  0.0 129.0 jit_solution(69708177307624733)
XLA Ops:
  1.3 126.3 %shard_map.77 = (bf16[2,16,3584]{2,1,0:T(8,128)(2,1)S(1)}, bf16[16,3584]{1,0:T(8,128)(2,1)S(1)}) custom-call(bf16[512,7168]{1,0:T(8,128)(2,1)} %pool.1, s32[1,128]{1,0:T(1,128)} %bitcast.1, bf16[128,7168]{1,0:T(8,128)(2,1)} %cot.1, bf16[2,16,3584]{2,1,0:T(8,128)(2,1)} %gate_up.1, bf16[16,3584]{1,0:T(8,128)(2,1)} %down.1, s32[1]{0:T(128)S(6)} %copy.10.exponent), custom_call_target="tpu_custom_call" | custom-call | tf_op jit(solution)/shard_map/pallas_call | solution.py:575
  127.6 0.7 copy.11
  128.3 0.6 copy.12

commit v6 on v5

--- a/solution.py
+++ b/solution.py
@@ -205,15 +205,6 @@
     b_next = same(w_block(z, rows_of(y), cols_b), z_next)
     b_back = same(w_block(z, rows_of(y), cols_b), z_back)
 
-    own_pool.wait()
-    pick(3, tok_x, slot(x, core))
-    dd_own_x = same(tok_x.at[slot(x, core), :], partner)
-    c_own.wait()
-    dd_own_c = same(tok_c.at[slot(x, core), :], partner)
-    next_pool.wait()
-    pick(1, picked.at[1], every)
-    back_pool.wait()
-    pick(2, picked.at[2], every)
 
     a_next.wait_recv()
     a_on = same(w_block(z, low_rows_of(yb), cols_a), y_next)
@@ -223,6 +214,11 @@
     b_on = same(w_block(zb, low_rows_of(y), cols_b), z_next)
     b_back.wait_recv()
     b_off = same(w_block(zn, high_rows_of(y), cols_b), z_back)
+
+    next_pool.wait()
+    pick(1, picked.at[1], every)
+    back_pool.wait()
+    pick(2, picked.at[2], every)
 
     a_on.wait_recv()
     a_off.wait_recv()
@@ -242,6 +238,11 @@
     x_pass = wire.send(via_x, tok_x.at[slot(xb, core), :], x_next)
     x_next_copy = wire.send(picked.at[1], tok_x.at[slot(x, core), :], x_next)
 
+    own_pool.wait()
+    pick(3, tok_x, slot(x, core))
+    dd_own_x = same(tok_x.at[slot(x, core), :], partner)
+    c_own.wait()
+    dd_own_c = same(tok_c.at[slot(x, core), :], partner)
     c_back.wait_recv()
     dd_c_n = same(tok_c.at[slot(xn, core), :], partner)
     c_next_a.wait_recv()

time: 129 us -> 129 us (level)
  no operation moved by 1% of the time
where the time goes in v6:
time: 129 us
  Pallas kernels  126 us (98%)
  local copies, waits for them, and re-layouts  1.34 us (1%)
  between operations  1.29 us (1%)
    pallas_call x1, Pallas kernels, per_device(): pl.pallas_call(kernel, out_shape=(jax.ShapeDtypeStruct(gate_up.shape, BF1...  126 us

profile of v6, /device:TPU:0, one launch (start us, length us, event | category | flops | bytes accessed | tf_op | source)
XLA Modules:
  0.0 129.0 jit_solution(7673263755732496653)
XLA Ops:
  1.3 126.4 %shard_map.77 = (bf16[2,16,3584]{2,1,0:T(8,128)(2,1)S(1)}, bf16[16,3584]{1,0:T(8,128)(2,1)S(1)}) custom-call(bf16[512,7168]{1,0:T(8,128)(2,1)} %pool.1, s32[1,128]{1,0:T(1,128)} %bitcast.1, bf16[128,7168]{1,0:T(8,128)(2,1)} %cot.1, bf16[2,16,3584]{2,1,0:T(8,128)(2,1)} %gate_up.1, bf16[16,3584]{1,0:T(8,128)(2,1)} %down.1, s32[1]{0:T(128)S(6)} %copy.10.exponent), custom_call_target="tpu_custom_call" | custom-call | tf_op jit(solution)/shard_map/pallas_call | solution.py:576
  127.7 0.7 copy.11
  128.4 0.6 copy.12

commit v7 on v6

--- a/solution.py
+++ b/solution.py
@@ -487,9 +487,9 @@
     grad_half(3, part_a, part_b)
     b_first(3)
     b_second(2)
+    grad_half(3, 0, part_a)
     b_sum(1)
     b_step(1)
-    grad_half(3, 0, part_a)
     ring_of_a[2].wait_recv()
     add3(sum_a, g_block(z, every_row, cols_a), ring_a.at[2])
 

time: 129 us -> 129 us (level)
  no operation moved by 1% of the time
where the time goes in v7:
time: 129 us
  Pallas kernels  126 us (98%)
  local copies, waits for them, and re-layouts  1.34 us (1%)
  between operations  1.29 us (1%)
    pallas_call x1, Pallas kernels, per_device(): pl.pallas_call(kernel, out_shape=(jax.ShapeDtypeStruct(gate_up.shape, BF1...  126 us

profile of v7, /device:TPU:0, one launch (start us, length us, event | category | flops | bytes accessed | tf_op | source)
XLA Modules:
  0.0 129.0 jit_solution(16708767278291002596)
XLA Ops:
  1.3 126.4 %shard_map.77 = (bf16[2,16,3584]{2,1,0:T(8,128)(2,1)S(1)}, bf16[16,3584]{1,0:T(8,128)(2,1)S(1)}) custom-call(bf16[512,7168]{1,0:T(8,128)(2,1)} %pool.1, s32[1,128]{1,0:T(1,128)} %bitcast.1, bf16[128,7168]{1,0:T(8,128)(2,1)} %cot.1, bf16[2,16,3584]{2,1,0:T(8,128)(2,1)} %gate_up.1, bf16[16,3584]{1,0:T(8,128)(2,1)} %down.1, s32[1]{0:T(128)S(6)} %copy.10.exponent), custom_call_target="tpu_custom_call" | custom-call | tf_op jit(solution)/shard_map/pallas_call | solution.py:576
  127.7 0.7 copy.11
  128.4 0.6 copy.12
